TPU v7x, 32 devices: a whole 2x2x4 slice. The times are simulated.
32 devices in a mesh: dp: 8 (over y, x, core), mp: 4 (over z).
Axes of the slice: x: 2, y: 2, z: 4, core: 2. Of those that a mesh axis runs over, the one named last changes fastest.
Arguments:
- token_ids: int32 [16], replicated, may hold values from 0 to 3071
- cache_lengths: int32 [16], P('dp'), may hold values from 1 to 512
- embedding: bfloat16 [3072, 12288], P(('dp', 'mp')), may hold values from -6 to 6
- ln_gain: float32 [12288], replicated, may hold values from 0.25 to 1.75
- query_weight: bfloat16 [12288, 6144], P('dp', 'mp'), may hold values from -0.0546875 to 0.0546875
- key_cache: bfloat16 [16, 512, 6144], P('dp', None, 'mp'), may hold values from -1000 to 1000
- value_cache: bfloat16 [16, 512, 6144], P('dp', None, 'mp'), may hold values from -6 to 6
- out_weight: bfloat16 [6144, 12288], P('mp', 'dp'), may hold values from -0.078125 to 0.078125
- final_gain: float32 [12288], replicated, may hold values from 0.25 to 1.75
Outputs:
- log_probs: float32 [16, 3072], P(None, ('dp', 'mp'))
All inputs are finite; a program needn't handle non-finite values.
Results may differ from a plain program's by a relative error of at most 0.00033.
Values may be sent and summed in bfloat16 or wider, within the bound.
A program may use at most 128 MiB of HBM per device.

v0:
```python
import jax
import jax.numpy as jnp
from jax import lax
from jax.sharding import PartitionSpec as P

HD = 128


def per_device(
    token_ids,
    cache_lengths,
    embedding,
    ln_gain,
    query_weight,
    key_cache,
    value_cache,
    out_weight,
    final_gain,
):
    voc_rows = embedding.shape[0]
    model_width = embedding.shape[1]
    vocab_start = lax.axis_index(("dp", "mp")) * voc_rows
    one_hot = (token_ids[:, None] - vocab_start == jnp.arange(voc_rows)[None, :]).astype(
        jnp.bfloat16
    )
    partial_rows = jnp.dot(one_hot, embedding, preferred_element_type=jnp.float32)
    seq_here = key_cache.shape[0]
    cache_len = key_cache.shape[1]
    cols_here = out_weight.shape[1]
    dp_index = lax.axis_index("dp")
    block_sums = lax.psum_scatter(
        partial_rows.astype(jnp.bfloat16), "dp", scatter_dimension=1, tiled=True
    )
    embedded_cols = lax.psum(block_sums, "mp").astype(jnp.float32)
    first_sum, first_sq = lax.psum(
        (jnp.sum(embedded_cols, axis=-1), jnp.sum(embedded_cols * embedded_cols, axis=-1)), "dp"
    )
    first_mean = first_sum / model_width
    first_var = first_sq / model_width - first_mean * first_mean
    ln_here = lax.dynamic_slice_in_dim(ln_gain, dp_index * cols_here, cols_here, 0)
    normed_cols = (
        ln_here * (embedded_cols - first_mean[:, None]) * lax.rsqrt(first_var[:, None] + 1e-05)
    ).astype(jnp.bfloat16)
    own_rows = lax.all_to_all(normed_cols, "dp", split_axis=0, concat_axis=1, tiled=True)
    query_sum = jnp.dot(
        own_rows,
        lax.all_gather(query_weight, "dp", axis=0, tiled=True),
        preferred_element_type=jnp.float32,
    )
    queries = (query_sum * HD ** (-0.5)).astype(jnp.bfloat16)
    heads_here = queries.shape[1] // HD
    head_query = queries.reshape(seq_here, heads_here, HD)
    key_heads = key_cache.reshape(seq_here, cache_len, heads_here, HD)
    value_heads = value_cache.reshape(seq_here, cache_len, heads_here, HD)
    scores = jnp.einsum("shd,sthd->sht", head_query, key_heads, preferred_element_type=jnp.float32)
    live_mask = jnp.arange(cache_len)[None, None, :] < cache_lengths[:, None, None]
    scores = jnp.where(live_mask, scores, jnp.float32(-1e30))
    row_top = jnp.max(scores, axis=-1, keepdims=True)
    exp_terms = jnp.exp(scores - row_top)
    weights = (exp_terms / jnp.sum(exp_terms, axis=-1, keepdims=True)).astype(jnp.bfloat16)
    attended = jnp.einsum("sht,sthd->shd", weights, value_heads, preferred_element_type=jnp.float32)
    attended = attended.astype(jnp.bfloat16).reshape(seq_here, heads_here * HD)
    every_seq = lax.all_gather(attended, "dp", axis=0, tiled=True)
    mixed_out = lax.psum(jnp.dot(every_seq, out_weight, preferred_element_type=jnp.float32), "mp")
    hidden = embedded_cols + mixed_out
    row_sum, row_sq = lax.psum((jnp.sum(hidden, axis=-1), jnp.sum(hidden * hidden, axis=-1)), "dp")
    row_mean = row_sum / model_width
    row_var = row_sq / model_width - row_mean * row_mean
    gain_here = lax.dynamic_slice_in_dim(final_gain, dp_index * cols_here, cols_here, 0)
    final_normed = (
        gain_here * (hidden - row_mean[:, None]) * lax.rsqrt(row_var[:, None] + 1e-05)
    ).astype(jnp.bfloat16)
    logits = lax.dot_general(
        lax.all_gather(final_normed, "dp", axis=1, tiled=True),
        embedding,
        (((1,), (1,)), ((), ())),
        preferred_element_type=jnp.float32,
    )
    local_top = jnp.max(logits, axis=-1)
    global_top = lax.pmax(local_top, ("dp", "mp"))
    total_exp = lax.psum(jnp.sum(jnp.exp(logits - global_top[:, None]), axis=-1), ("dp", "mp"))
    return logits - global_top[:, None] - jnp.log(total_exp)[:, None]


def solution(mesh):
    return jax.shard_map(
        per_device,
        mesh=mesh,
        in_specs=(
            P(),
            P("dp"),
            P(("dp", "mp"), None),
            P(),
            P("dp", "mp"),
            P("dp", None, "mp"),
            P("dp", None, "mp"),
            P("mp", "dp"),
            P(),
        ),
        out_specs=P(None, ("dp", "mp")),
        check_vma=False,
    )
```

profile of v0, /device:TPU:0, one launch (start us, length us, event | category | flops | bytes accessed | tf_op | source)
XLA Modules:
  0.0 406.1 jit_solution(14732259672830846114)
XLA Ops:
  6.5 0.8 broadcast_subtract_fusion
  7.3 0.9 copy-done
  8.2 1.2 convolution_convert_fusion
  11.0 36.0 %reduce-scatter.2.cloned.1.call-done = bf16[16,1536]{1,0:T(8,128)(2,1)} async-done(((bf16[16,12288]{1,0:T(8,128)(2,1)}), bf16[16,1536]{1,0:T(8,128)(2,1)}) %reduce-scatter.2.cloned.1.call-update) | async-done | bytes 49168 | tf_op jit(solution)/shard_map/reduce_scatter | solution.py:31
  47.0 19.9 %psum.49 = bf16[16,1536]{1,0:T(8,128)(2,1)S(1)} all-reduce(bf16[16,1536]{1,0:T(8,128)(2,1)} %reduce-scatter.2.cloned.1.call-done), channel_id=1, replica_groups=mesh['dp'=8,'mp'=4] {'mp'}, use_global_device_ids=true, to_apply=%region_1.0 | all-reduce | flops 24576 | bytes 98304 | tf_op jit(solution)/shard_map/psum | solution.py:34
  67.1 12.8 %all-reduce.1 = (f32[16]{0:T(128)S(1)}, f32[16]{0:T(128)S(1)}) all-reduce(f32[16]{0:T(128)S(1)} %get-tuple-element.8, f32[16]{0:T(128)S(1)} %get-tuple-element.7), channel_id=1, replica_groups=mesh['dp'=8,'mp'=4] {'dp'}, use_global_device_ids=true, to_apply=%region_5.0 | all-reduce | flops 32 | bytes 256 | tf_op jit(solution)/shard_map/psum | solution.py:35
  80.6 3.3 all-to-all-start
  84.1 4.7 %copy.14 = bf16[2,512,1536]{1,2,0:T(8,128)(2,1)} copy(bf16[2,512,1536]{2,1,0:T(8,128)(2,1)} %param.14) | data formatting | bytes 6291456 | tf_op args[5]
  88.8 4.7 %copy.15 = bf16[2,512,1536]{1,2,0:T(8,128)(2,1)} copy(bf16[2,512,1536]{2,1,0:T(8,128)(2,1)} %param.15) | data formatting | bytes 6291456 | tf_op args[6]
  93.4 135.6 %all-gather.3.cloned.1.call-done = bf16[12288,1536]{1,0:T(8,128)(2,1)} async-done(((bf16[1536,1536]{1,0:T(8,128)(2,1)}), bf16[12288,1536]{1,0:T(8,128)(2,1)}) %all-gather.3.cloned.1.call-update) | async-done | bytes 37748752 | tf_op jit(solution)/shard_map/all_gather | solution.py:47
  229.1 14.3 %fusion.2 = bf16[2,1536]{1,0:T(2,128)(2,1)S(1)} fusion(bf16[2,12288]{1,0:T(2,128)(2,1)S(1)} %bitcast.29, bf16[12288,1536]{1,0:T(8,128)(2,1)} %all-gather.3.cloned.1.call-done), kind=kOutput, calls=%fused_computation.4 | convolution fusion | flops 75503616 | bytes 37804032 | tf_op jit(solution)/shard_map/dot_general | solution.py:45
  243.4 2.4 fusion.20
  246.0 2.8 fusion.12
  248.8 9.1 %all-gather = bf16[8,2,1536]{2,1,0:T(2,128)(2,1)S(1)} all-gather(bf16[1,2,1536]{2,1,0:T(2,128)(2,1)S(1)} %reshape.56), channel_id=1, replica_groups=mesh['dp'=8,'mp'=4] {'dp'}, dimensions={0}, use_global_device_ids=true | all-gather | bytes 55296 | tf_op jit(solution)/shard_map/all_gather | solution.py:63
  258.0 3.7 fusion.21
  261.7 0.8 dynamic_slice.6
  262.5 33.8 %all-reduce.4.cloned.1.call-done = f32[16,1536]{1,0:T(8,128)} async-done(((f32[16,1536]{1,0:T(8,128)}), f32[16,1536]{1,0:T(8,128)}) %all-reduce.4.cloned.1.call-update) | async-done | bytes 98320 | tf_op jit(solution)/shard_map/psum | solution.py:64
  296.3 1.0 fusion.14
  297.3 11.8 %all-reduce = (f32[16]{0:T(128)S(1)}, f32[16]{0:T(128)S(1)}) all-reduce(f32[16]{0:T(128)S(1)} %get-tuple-element.6, f32[16]{0:T(128)S(1)} %get-tuple-element.5), channel_id=1, replica_groups=mesh['dp'=8,'mp'=4] {'dp'}, use_global_device_ids=true, to_apply=%region_12.13 | all-reduce | flops 32 | bytes 256 | tf_op jit(solution)/shard_map/psum | solution.py:66
  309.2 1.0 multiply_convert_fusion
  310.1 9.5 %all_gather.11 = bf16[16,12288]{1,0:T(8,128)(2,1)S(1)} all-gather(bf16[16,1536]{1,0:T(8,128)(2,1)S(1)} %multiply_convert_fusion), channel_id=1, replica_groups=mesh['dp'=8,'mp'=4] {'dp'}, dimensions={1}, use_global_device_ids=true | all-gather | bytes 442368 | tf_op jit(solution)/shard_map/all_gather | solution.py:74
  319.7 0.8 fusion.19
  320.5 39.2 %pmax.7 = f32[16]{0:T(128)S(1)} all-reduce(f32[16]{0:T(128)S(1)} %get-tuple-element.17), channel_id=1, replica_groups=mesh['dp'=8,'mp'=4] {'dp','mp'}, use_global_device_ids=true, to_apply=%region_14.15 | all-reduce | flops 16 | bytes 128 | tf_op jit(solution)/shard_map/pmax | solution.py:80
  359.9 39.0 %psum.55 = f32[16]{0:T(128)S(1)} all-reduce(f32[16]{0:T(128)S(1)} %exponential_reduce_fusion), channel_id=1, replica_groups=mesh['dp'=8,'mp'=4] {'dp','mp'}, use_global_device_ids=true, to_apply=%region_16.17 | all-reduce | flops 16 | bytes 128 | tf_op jit(solution)/shard_map/psum | solution.py:81
  (25 shorter events, 3.7 us)
Async XLA Ops:
  6.5 1.7 copy-start
  6.5 40.5 %reduce-scatter.2.cloned.1.call-start = ((), (), s32[]{:S(2)}) async-start(), calls=%async_computation.2 | async-start | bytes 442368 | tf_op jit(solution)/shard_map/reduce_scatter | solution.py:31
  9.5 74.5 %copy-start.1 = (s32[2]{0:T(128)S(1)}, s32[2]{0:T(128)}, u32[]{:S(2)}) copy-start(s32[2]{0:T(128)} %param.10) | copy-start | bytes 28
  9.5 219.6 %all-gather.3.cloned.1.call-start = ((), (), s32[]{:S(2)}) async-start(), calls=%async_computation.3 | async-start | bytes 42467328 | tf_op jit(solution)/shard_map/all_gather | solution.py:47
  80.6 12.9 %all-to-all-start = ((bf16[8,2,1536]{2,1,0:T(2,128)(2,1)}), bf16[8,2,1536]{2,1,0:T(2,128)(2,1)S(1)}, u32[]{:S(2)}, u32[]{:S(2)}) async-start(bf16[8,2,1536]{2,1,0:T(2,128)(2,1)} %all_to_all.14), calls=%async_computation.1 | async-start | bytes 98304 | tf_op jit(solution)/shard_map/all_to_all | solution.py:44
  83.9 212.4 %all-reduce.4.cloned.1.call-start = ((), (), s32[]{:S(2)}) async-start(), calls=%async_computation.4 | async-start | bytes 196608 | tf_op jit(solution)/shard_map/psum | solution.py:64
Sparse Core Ops, SparseCore 0:
  10.4 36.5 reduce-scatter.1
  48.9 180.1 all-gather.2
  261.8 34.4 all-reduce.3
where the time goes:
time: 407 us; the launch traced here: 406 us
  waiting for transfers between devices  206 us (51%)
  blocking collectives  141 us (35%)
  matrix products  25.2 us (6%)
  between operations  13.2 us (3%)
  local copies, waits for them, and re-layouts  12.6 us (3%)
  other arithmetic  4.18 us (1%)
    all_gather x1, waiting for transfers between devices, per_device(): lax.all_gather(query_weight, 'dp', axis=0, tiled=True)  136 us
    pmax x1, blocking collectives, per_device(): global_top = lax.pmax(local_top, ('dp', 'mp'))  39.2 us
    psum x1, blocking collectives, per_device(): lax.psum(jnp.sum(jnp.exp(logits - global_top[:, None]), axis=-1), ('dp',...  39 us
    reduce_scatter x1, waiting for transfers between devices, per_device(): lax.psum_scatter(partial_rows.astype(jnp.bfloat16), 'dp', scatter_dimensi...  36 us
    psum x1, waiting for transfers between devices, per_device(): lax.psum(jnp.dot(every_seq, out_weight, preferred_element_type=jnp.float3...  33.8 us
    psum x1, blocking collectives, per_device(): embedded_cols = lax.psum(block_sums, 'mp').astype(jnp.float32)  19.9 us
    dot_general x1, matrix products, per_device(): jnp.dot(own_rows, lax.all_gather(query_weight, 'dp', axis=0, tiled=True),...  14.3 us
    psum x1, blocking collectives, per_device(): lax.psum((jnp.sum(embedded_cols, axis=-1), jnp.sum(embedded_cols * embedd...  12.8 us
  transfers between devices with their start and end apart: 4, of which 3 were waited for; matrix products, arithmetic and copies ran while one was open for 3% of the time, Pallas kernels for 0%

commit v1 on v0

v1 whole, which is shorter than its diff:
```python
import functools

import jax
import jax.numpy as jnp
from jax import lax
from jax.experimental import pallas as pl
from jax.experimental.pallas import tpu as pltpu
from jax.sharding import PartitionSpec as P

HD = 128
LANES = 128
EPS = 1e-05
MESH = pl.DeviceIdType.MESH
F32 = jnp.float32
BF16 = jnp.bfloat16


def to_lanes(column):
    rows = column.shape[0]
    row = lax.broadcasted_iota(jnp.int32, (rows, LANES), 0)
    lane = lax.broadcasted_iota(jnp.int32, (rows, LANES), 1)
    return jnp.sum(jnp.where(row == lane, column, 0.0), axis=0, keepdims=True)


def to_column(lanes, rows):
    row = lax.broadcasted_iota(jnp.int32, (rows, LANES), 0)
    lane = lax.broadcasted_iota(jnp.int32, (rows, LANES), 1)
    return jnp.sum(jnp.where(row == lane, lanes, 0.0), axis=1, keepdims=True)


def kernel(
    dp,
    mp,
    tokens,
    lengths,
    emb_hbm,
    ln_hbm,
    wq_hbm,
    key_hbm,
    val_hbm,
    wo_hbm,
    fg_hbm,
    out,
    emb,
    ln_gain,
    wq,
    keys,
    vals,
    wo,
    fin_gain,
    emb_send,
    emb_recv,
    emb_z,
    stat1,
    embedded,
    q_part,
    q_recv,
    att,
    o_part,
    o_recv,
    hid,
    stat2,
    fin,
    top,
    load_sem,
    emb_s,
    emb_r,
    z_s,
    z_r,
    st1_s,
    st1_r,
    q_s,
    q_r,
    att_s,
    att_r,
    o_s,
    o_r,
    hid_s,
    hid_r,
    st2_s,
    st2_r,
    fin_s,
    fin_r,
    top_s,
    top_r,
):
    d = lax.axis_index("dp")
    m = lax.axis_index("mp")
    n = dp * mp
    me = d * mp + m
    voc, width = emb.shape
    cols = wo.shape[1]
    seqs = dp * keys.shape[0]
    seq_here = keys.shape[0]
    heads_cols = wq.shape[1]
    rows = seqs // mp

    def load(src, dst, index):
        return pltpu.make_async_copy(src, dst, load_sem.at[index])

    here = pl.ds(pl.multiple_of(d * cols, LANES), cols)
    loads = [
        load(emb_hbm, emb, 0),
        load(ln_hbm.at[here], ln_gain, 1),
        load(wq_hbm, wq, 2),
        load(key_hbm, keys, 3),
        load(val_hbm, vals, 4),
        load(wo_hbm, wo, 5),
        load(fg_hbm.at[here], fin_gain, 6),
    ]
    for copy in loads:
        copy.start()

    barrier = pltpu.get_barrier_semaphore()

    def greet(k, carry):
        other = lax.rem(me + k, n)
        pl.semaphore_signal(
            barrier, inc=1, device_id=(other // mp, lax.rem(other, mp)), device_id_type=MESH
        )
        return carry

    lax.fori_loop(1, n, greet, 0)

    def over_dp(src, dst, send, recv, k):
        other = lax.rem(d + k, dp)
        return pltpu.make_async_remote_copy(
            src_ref=src(other),
            dst_ref=dst.at[d],
            send_sem=send.at[other],
            recv_sem=recv.at[d],
            device_id=(other, m),
            device_id_type=MESH,
        )

    def from_dp(dst, send, recv, k):
        other = lax.rem(d + k, dp)
        return pltpu.make_async_remote_copy(
            src_ref=dst.at[other],
            dst_ref=dst.at[other],
            send_sem=send.at[other],
            recv_sem=recv.at[other],
            device_id=(other, m),
            device_id_type=MESH,
        )

    def over_mp(src, dst, send, recv, k):
        other = lax.rem(m + k, mp)
        return pltpu.make_async_remote_copy(
            src_ref=src(other),
            dst_ref=dst.at[m],
            send_sem=send.at[other],
            recv_sem=recv.at[m],
            device_id=(d, other),
            device_id_type=MESH,
        )

    def from_mp(dst, send, recv, k):
        other = lax.rem(m + k, mp)
        return pltpu.make_async_remote_copy(
            src_ref=dst.at[other],
            dst_ref=dst.at[other],
            send_sem=send.at[other],
            recv_sem=recv.at[other],
            device_id=(d, other),
            device_id_type=MESH,
        )

    def small(buf, send, recv, other, slot):
        return pltpu.make_async_remote_copy(
            src_ref=buf.at[slot],
            dst_ref=buf.at[slot],
            send_sem=send.at[other],
            recv_sem=recv.at[slot],
            device_id=(other // mp, lax.rem(other, mp)),
            device_id_type=MESH,
        )

    def send_small(buf, send, recv):
        def body(k, carry):
            small(buf, send, recv, lax.rem(me + k, n), me).start()
            return carry

        lax.fori_loop(1, n, body, 0)

    def wait_small(buf, send, recv):
        def body(k, carry):
            other = lax.rem(me + k, n)
            small(buf, send, recv, other, other).wait_recv()
            return carry

        lax.fori_loop(1, n, body, 0)

    def sent_small(buf, send, recv):
        def body(k, carry):
            small(buf, send, recv, lax.rem(me + k, n), me).wait_send()
            return carry

        lax.fori_loop(1, n, body, 0)

    row = lax.broadcasted_iota(jnp.int32, (seqs, voc), 0)
    token = jnp.zeros((seqs, voc), jnp.int32)
    for s in range(seqs):
        token = jnp.where(row == s, tokens[s], token)
    voc_id = lax.broadcasted_iota(jnp.int32, (seqs, voc), 1) + me * voc
    one_hot = jnp.where(token == voc_id, 1.0, 0.0).astype(BF16)
    loads[0].wait()
    total = jnp.zeros((seqs, 1), F32)
    for j in range(dp):
        block = jnp.dot(
            one_hot, emb[:, j * cols : (j + 1) * cols], preferred_element_type=F32
        )
        emb_send[j] = block.astype(BF16)
        total = total + jnp.sum(block, axis=1, keepdims=True)
    pl.semaphore_wait(barrier, n - 1)
    sends = [over_dp(lambda j: emb_send.at[j], emb_recv, emb_s, emb_r, k) for k in range(1, dp)]
    for copy in sends:
        copy.start()
    mean = total * (1.0 / width)
    var = jnp.zeros((seqs, 1), F32)
    for j in range(dp):
        off = emb_send[j].astype(F32) - mean
        var = var + jnp.sum(off * off, axis=1, keepdims=True)
    stat1[me] = jnp.concatenate([to_lanes(mean), to_lanes(var * (1.0 / width))], axis=0)
    send_small(stat1, st1_s, st1_r)

    block_sum = emb_send[d].astype(F32)
    for k in range(1, dp):
        from_dp(emb_recv, emb_s, emb_r, k).wait_recv()
        block_sum = block_sum + emb_recv[lax.rem(d + k, dp)].astype(F32)
    emb_z[m] = block_sum.astype(BF16)
    z_sends = [over_mp(lambda j: emb_z.at[m], emb_z, z_s, z_r, k) for k in range(1, mp)]
    for copy in z_sends:
        copy.start()
    for copy in loads[1:]:
        copy.wait()
    wait_small(stat1, st1_s, st1_r)
    stats = jnp.sum(stat1[...], axis=0)
    first_mean = to_column(stats[0:1], seqs)
    first_scale = lax.rsqrt(to_column(stats[1:2], seqs) + EPS)
    for k in range(1, mp):
        from_mp(emb_z, z_s, z_r, k).wait_recv()
        block_sum = block_sum + emb_z[lax.rem(m + k, mp)].astype(F32)
    for j in range(mp):
        embedded[j] = block_sum[j * rows : (j + 1) * rows]

    gain = ln_gain[...].reshape(1, cols)
    normed = (gain * (block_sum - first_mean) * first_scale).astype(BF16)
    part = jnp.dot(normed, wq[...], preferred_element_type=F32)
    for j in range(dp):
        q_part[j] = part[j * seq_here : (j + 1) * seq_here]
    q_sends = [over_dp(lambda j: q_part.at[j], q_recv, q_s, q_r, k) for k in range(1, dp)]
    for copy in q_sends:
        copy.start()
    query_sum = q_part[d]
    for k in range(1, dp):
        from_dp(q_recv, q_s, q_r, k).wait_recv()
        query_sum = query_sum + q_recv[lax.rem(d + k, dp)]
    queries = (query_sum * HD ** (-0.5)).astype(BF16).astype(F32)

    heads = heads_cols // HD
    head_rows = -(-heads // 16) * 16
    cache_len = keys.shape[1]
    head_row = lax.broadcasted_iota(jnp.int32, (head_rows, heads_cols), 0)
    head_col = lax.broadcasted_iota(jnp.int32, (head_rows, heads_cols), 1)
    start = head_row * HD
    diagonal = (head_col >= start) & (head_col < start + HD)
    place = lax.broadcasted_iota(jnp.int32, (head_rows, cache_len), 1)
    rows_out = []
    for s in range(seq_here):
        spread = jnp.where(diagonal, queries[s : s + 1], 0.0).astype(BF16)
        scores = lax.dot_general(
            spread, keys[s], (((1,), (1,)), ((), ())), preferred_element_type=F32
        )
        scores = jnp.where(place < lengths[s], scores, F32(-1e30))
        exp_terms = jnp.exp(scores - jnp.max(scores, axis=-1, keepdims=True))
        weights = (exp_terms / jnp.sum(exp_terms, axis=-1, keepdims=True)).astype(BF16)
        mixed = jnp.dot(weights, vals[s], preferred_element_type=F32)
        rows_out.append(jnp.sum(jnp.where(diagonal, mixed, 0.0), axis=0, keepdims=True))
    att[d] = jnp.concatenate(rows_out, axis=0).astype(BF16)
    att_sends = [over_dp(lambda j: att.at[d], att, att_s, att_r, k) for k in range(1, dp)]
    for copy in att_sends:
        copy.start()
    for k in range(1, dp):
        from_dp(att, att_s, att_r, k).wait_recv()
    every = jnp.concatenate([att[j].astype(F32) for j in range(dp)], axis=0).astype(BF16)

    part = jnp.dot(every, wo[...], preferred_element_type=F32)
    for j in range(mp):
        o_part[j] = part[j * rows : (j + 1) * rows]
    o_sends = [over_mp(lambda j: o_part.at[j], o_recv, o_s, o_r, k) for k in range(1, mp)]
    for copy in o_sends:
        copy.start()
    mixed = o_part[m]
    for k in range(1, mp):
        from_mp(o_recv, o_s, o_r, k).wait_recv()
        mixed = mixed + o_recv[lax.rem(m + k, mp)]
    hidden = embedded[m] + mixed
    hid[m] = hidden
    hid_sends = [over_mp(lambda j: hid.at[m], hid, hid_s, hid_r, k) for k in range(1, mp)]
    for copy in hid_sends:
        copy.start()
    stat2[me] = jnp.concatenate(
        [
            to_lanes(jnp.sum(hidden, axis=1, keepdims=True)),
            to_lanes(jnp.sum(hidden * hidden, axis=1, keepdims=True)),
        ],
        axis=0,
    )
    send_small(stat2, st2_s, st2_r)
    for k in range(1, mp):
        from_mp(hid, hid_s, hid_r, k).wait_recv()
    wait_small(stat2, st2_s, st2_r)
    gain = fin_gain[...].reshape(1, cols)
    pieces = []
    for j in range(mp):
        stats = stat2[j]
        for i in range(1, dp):
            stats = stats + stat2[i * mp + j]
        stats = stats * (1.0 / width)
        row_mean = to_column(stats[0:1], rows)
        row_var = to_column(stats[1:2], rows) - row_mean * row_mean
        pieces.append(gain * (hid[j] - row_mean) * lax.rsqrt(row_var + EPS))
    fin[d] = jnp.concatenate(pieces, axis=0).astype(BF16)
    fin_sends = [over_dp(lambda j: fin.at[d], fin, fin_s, fin_r, k) for k in range(1, dp)]
    for copy in fin_sends:
        copy.start()

    def block_logits(j):
        features = pl.ds(pl.multiple_of(j * cols, LANES), cols)
        return lax.dot_general(
            fin[j], emb[:, features], (((1,), (1,)), ((), ())), preferred_element_type=F32
        )

    logits = block_logits(d)
    for k in range(1, dp):
        from_dp(fin, fin_s, fin_r, k).wait_recv()
        logits = logits + block_logits(lax.rem(d + k, dp))
    local_top = jnp.max(logits, axis=-1, keepdims=True)
    local_sum = jnp.sum(jnp.exp(logits - local_top), axis=-1, keepdims=True)
    top[me] = jnp.concatenate([to_lanes(local_top), to_lanes(local_sum)], axis=0)
    send_small(top, top_s, top_r)

    for copy in sends + z_sends + q_sends + att_sends + o_sends + hid_sends + fin_sends:
        copy.wait_send()
    sent_small(stat1, st1_s, st1_r)
    sent_small(stat2, st2_s, st2_r)
    wait_small(top, top_s, top_r)
    tops = top[:, 0:1, :]
    global_top = jnp.max(tops, axis=0)
    global_sum = jnp.sum(top[:, 1:2, :] * jnp.exp(tops - global_top[None]), axis=0)
    top_col = to_column(global_top, seqs)
    sum_col = to_column(global_sum, seqs)
    out[...] = logits - top_col - jnp.log(sum_col)
    sent_small(top, top_s, top_r)


def per_device(
    dp,
    mp,
    token_ids,
    cache_lengths,
    embedding,
    ln_gain,
    query_weight,
    key_cache,
    value_cache,
    out_weight,
    final_gain,
):
    n = dp * mp
    seqs = token_ids.shape[0]
    seq_here = key_cache.shape[0]
    cols = out_weight.shape[1]
    head_cols = query_weight.shape[1]
    rows = seqs // mp
    any_space = pl.BlockSpec(memory_space=pl.ANY)
    smem = pl.BlockSpec(memory_space=pltpu.SMEM)
    dma = pltpu.SemaphoreType.DMA
    pairs = [dp, mp, n, dp, dp, mp, mp, n, dp, n]
    return pl.pallas_call(
        functools.partial(kernel, dp, mp),
        out_shape=jax.ShapeDtypeStruct((seqs, embedding.shape[0]), F32),
        in_specs=[smem, smem] + [any_space] * 7,
        out_specs=pl.BlockSpec(memory_space=pltpu.VMEM),
        scratch_shapes=[
            pltpu.VMEM(embedding.shape, BF16),
            pltpu.VMEM((cols,), F32),
            pltpu.VMEM(query_weight.shape, BF16),
            pltpu.VMEM(key_cache.shape, BF16),
            pltpu.VMEM(value_cache.shape, BF16),
            pltpu.VMEM(out_weight.shape, BF16),
            pltpu.VMEM((cols,), F32),
            pltpu.VMEM((dp, seqs, cols), BF16),
            pltpu.VMEM((dp, seqs, cols), BF16),
            pltpu.VMEM((mp, seqs, cols), BF16),
            pltpu.VMEM((n, 2, LANES), F32),
            pltpu.VMEM((mp, rows, cols), F32),
            pltpu.VMEM((dp, seq_here, head_cols), F32),
            pltpu.VMEM((dp, seq_here, head_cols), F32),
            pltpu.VMEM((dp, seq_here, head_cols), BF16),
            pltpu.VMEM((mp, rows, cols), F32),
            pltpu.VMEM((mp, rows, cols), F32),
            pltpu.VMEM((mp, rows, cols), F32),
            pltpu.VMEM((n, 2, LANES), F32),
            pltpu.VMEM((dp, seqs, cols), BF16),
            pltpu.VMEM((n, 2, LANES), F32),
            dma((7,)),
        ]
        + [dma((size,)) for size in pairs for _ in range(2)],
        compiler_params=pltpu.CompilerParams(
            collective_id=0, has_side_effects=True, vmem_limit_bytes=60 * 1024 * 1024
        ),
    )(
        token_ids,
        cache_lengths,
        embedding,
        ln_gain,
        query_weight,
        key_cache,
        value_cache,
        out_weight,
        final_gain,
    )


def solution(mesh):
    return jax.shard_map(
        functools.partial(per_device, mesh.shape["dp"], mesh.shape["mp"]),
        mesh=mesh,
        in_specs=(
            P(),
            P("dp"),
            P(("dp", "mp"), None),
            P(),
            P("dp", "mp"),
            P("dp", None, "mp"),
            P("dp", None, "mp"),
            P("mp", "dp"),
            P(),
        ),
        out_specs=P(None, ("dp", "mp")),
        check_vma=False,
    )
```

time: 407 us -> 57.3 us (0.14)
  waiting for transfers between devices: 206 us -> 0 us
  blocking collectives: 141 us -> 0 us
  Pallas kernels: 0 us -> 55.8 us
  matrix products: 25.2 us -> 0 us
  between operations: 13.2 us -> 0.01 us
  local copies, waits for them, and re-layouts: 12.6 us -> 1.3 us
  other arithmetic: 4.18 us -> 0 us
    all_gather x1 -> x0, waiting for transfers between devices: 136 us -> none  [per_device(): lax.all_gather(query_weight, 'dp', axis=0, tiled=True)]
    psum x4 -> x0, blocking collectives: 83.5 us -> none  [the longest x1 39 us: per_device(): lax.psum(jnp.sum(jnp.exp(logits - global_top[:, None]), axis=-1), ('dp',...]
    pallas_call x0 -> x1, Pallas kernels: none -> 55.8 us  [per_device(): pl.pallas_call(functools.partial(kernel, dp, mp), out_shape=jax.ShapeDtyp...]
    pmax x1 -> x0, blocking collectives: 39.2 us -> none  [per_device(): global_top = lax.pmax(local_top, ('dp', 'mp'))]
    reduce_scatter x1 -> x0, waiting for transfers between devices: 36 us -> none  [per_device(): lax.psum_scatter(partial_rows.astype(jnp.bfloat16), 'dp', scatter_dimensi...]
    psum x1 -> x0, waiting for transfers between devices: 33.8 us -> none  [per_device(): lax.psum(jnp.dot(every_seq, out_weight, preferred_element_type=jnp.float3...]
    dot_general x6 -> x0, matrix products: 25.2 us -> none  [the longest x1 14.3 us: per_device(): jnp.dot(own_rows, lax.all_gather(query_weight, 'dp', axis=0, tiled=True),...]
    all_gather x2 -> x0, blocking collectives: 18.7 us -> none  [the longest x1 9.54 us: per_device(): lax.all_gather(final_normed, 'dp', axis=1, tiled=True)]
  transfers between devices with their start and end apart: 4 -> 0, of which waited for: 3 -> 0; matrix products, arithmetic and copies ran while one was open for 3% -> 0% of each run, Pallas kernels for 0% -> 0%
where the time goes in v1:
time: 57.3 us; the launch traced here: 57.1 us
  Pallas kernels  55.8 us (97%)
  local copies, waits for them, and re-layouts  1.3 us (2%)
    pallas_call x1, Pallas kernels, per_device(): pl.pallas_call(functools.partial(kernel, dp, mp), out_shape=jax.ShapeDtyp...  55.8 us
    unnamed x1, local copies, waits for them, and re-layouts  1.3 us

profile of v1, /device:TPU:0, one launch (start us, length us, event | category | flops | bytes accessed | tf_op | source)
XLA Modules:
  0.0 57.1 jit_solution(289639186599031469)
XLA Ops:
  0.0 55.8 %shard_map.91 = f32[16,96]{1,0:T(8,128)} custom-call(s32[16]{0:T(128)} %tokens.1, s32[2]{0:T(128)} %lengths.1, bf16[96,12288]{1,0:T(8,128)(2,1)} %emb_hbm.1, f32[12288]{0:T(1024)} %ln_hbm.1, bf16[1536,1536]{1,0:T(8,128)(2,1)} %wq_hbm.1, bf16[2,512,1536]{2,1,0:T(8,128)(2,1)} %key_hbm.1, bf16[2,512,1536]{2,1,0:T(8,128)(2,1)} %val_hbm.1, ...), custom_call_target="tpu_custom_call" | custom-call | tf_op jit(solution)/shard_map/pallas_call | solution.py:381
  55.8 1.3 %copy.11 = f32[16,96]{1,0:T(8,128)} copy(f32[16,96]{1,0:T(8,128)} %shard_map.91) | data formatting | bytes 12288

commit v2 on v1

--- a/solution.py
+++ b/solution.py
@@ -9,6 +9,7 @@
 
 HD = 128
 LANES = 128
+CHUNKS = 3
 EPS = 1e-05
 MESH = pl.DeviceIdType.MESH
 F32 = jnp.float32
@@ -62,6 +63,8 @@
     stat2,
     fin,
     top,
+    hop,
+    met,
     load_sem,
     emb_s,
     emb_r,
@@ -113,14 +116,22 @@
 
     barrier = pltpu.get_barrier_semaphore()
 
-    def greet(k, carry):
-        other = lax.rem(me + k, n)
-        pl.semaphore_signal(
-            barrier, inc=1, device_id=(other // mp, lax.rem(other, mp)), device_id_type=MESH
-        )
-        return carry
-
-    lax.fori_loop(1, n, greet, 0)
+    def signal(sem, row, column):
+        pl.semaphore_signal(sem, inc=1, device_id=(row, column), device_id_type=MESH)
+
+    def signal_line(sem):
+        @pl.when(m > 0)
+        def _():
+            signal(sem, d, m - 1)
+
+        @pl.when(m < mp - 1)
+        def _():
+            signal(sem, d, m + 1)
+
+    line = jnp.where(m > 0, 1, 0) + jnp.where(m < mp - 1, 1, 0)
+    for k in range(1, dp):
+        signal(barrier, lax.rem(d + k, dp), m)
+    signal_line(barrier)
 
     def over_dp(src, dst, send, recv, k):
         other = lax.rem(d + k, dp)
@@ -205,44 +216,70 @@
     voc_id = lax.broadcasted_iota(jnp.int32, (seqs, voc), 1) + me * voc
     one_hot = jnp.where(token == voc_id, 1.0, 0.0).astype(BF16)
     loads[0].wait()
+    chunks = emb_send.shape[0]
+    wide = cols // chunks
     total = jnp.zeros((seqs, 1), F32)
-    for j in range(dp):
-        block = jnp.dot(
-            one_hot, emb[:, j * cols : (j + 1) * cols], preferred_element_type=F32
-        )
-        emb_send[j] = block.astype(BF16)
-        total = total + jnp.sum(block, axis=1, keepdims=True)
-    pl.semaphore_wait(barrier, n - 1)
-    sends = [over_dp(lambda j: emb_send.at[j], emb_recv, emb_s, emb_r, k) for k in range(1, dp)]
+    for i in range(chunks):
+        for j in range(dp):
+            begin = j * cols + i * wide
+            block = jnp.dot(
+                one_hot, emb[:, begin : begin + wide], preferred_element_type=F32
+            )
+            emb_send[i, j] = block.astype(BF16)
+            total = total + jnp.sum(block, axis=1, keepdims=True)
+    pl.semaphore_wait(barrier, dp - 1 + line)
+    if mp > 2:
+        signal_line(hop.at[0])
+    sends = [
+        over_dp(lambda j: emb_send.at[i, j], emb_recv.at[i], emb_s.at[i], emb_r.at[i], k)
+        for i in range(chunks)
+        for k in range(1, dp)
+    ]
     for copy in sends:
         copy.start()
     mean = total * (1.0 / width)
     var = jnp.zeros((seqs, 1), F32)
-    for j in range(dp):
-        off = emb_send[j].astype(F32) - mean
-        var = var + jnp.sum(off * off, axis=1, keepdims=True)
+    for i in range(chunks):
+        for j in range(dp):
+            off = emb_send[i, j].astype(F32) - mean
+            var = var + jnp.sum(off * off, axis=1, keepdims=True)
     stat1[me] = jnp.concatenate([to_lanes(mean), to_lanes(var * (1.0 / width))], axis=0)
-    send_small(stat1, st1_s, st1_r)
-
-    block_sum = emb_send[d].astype(F32)
+    for step in range(mp - 2):
+        pl.semaphore_wait(hop.at[step], line)
+        if step + 1 < mp - 2:
+            signal_line(hop.at[step + 1])
     for k in range(1, dp):
-        from_dp(emb_recv, emb_s, emb_r, k).wait_recv()
-        block_sum = block_sum + emb_recv[lax.rem(d + k, dp)].astype(F32)
-    emb_z[m] = block_sum.astype(BF16)
-    z_sends = [over_mp(lambda j: emb_z.at[m], emb_z, z_s, z_r, k) for k in range(1, mp)]
-    for copy in z_sends:
-        copy.start()
+        signal(met, lax.rem(d + k, dp), m)
+
+    block_sums = []
+    z_sends = []
+    for i in range(chunks):
+        part_sum = emb_send[i, d].astype(F32)
+        for k in range(1, dp):
+            from_dp(emb_recv.at[i], emb_s.at[i], emb_r.at[i], k).wait_recv()
+            part_sum = part_sum + emb_recv[i, lax.rem(d + k, dp)].astype(F32)
+        emb_z[i, m] = part_sum.astype(BF16)
+        block_sums.append(part_sum)
+        for k in range(1, mp):
+            copy = over_mp(lambda j: emb_z.at[i, m], emb_z.at[i], z_s.at[i], z_r.at[i], k)
+            copy.start()
+            z_sends.append(copy)
+        if i == 0:
+            pl.semaphore_wait(met, dp - 1)
+            send_small(stat1, st1_s, st1_r)
     for copy in loads[1:]:
         copy.wait()
+    for i in range(chunks):
+        for k in range(1, mp):
+            from_mp(emb_z.at[i], z_s.at[i], z_r.at[i], k).wait_recv()
+            block_sums[i] = block_sums[i] + emb_z[i, lax.rem(m + k, mp)].astype(F32)
+    block_sum = jnp.concatenate(block_sums, axis=1)
+    for j in range(mp):
+        embedded[j] = block_sum[j * rows : (j + 1) * rows]
     wait_small(stat1, st1_s, st1_r)
     stats = jnp.sum(stat1[...], axis=0)
     first_mean = to_column(stats[0:1], seqs)
     first_scale = lax.rsqrt(to_column(stats[1:2], seqs) + EPS)
-    for k in range(1, mp):
-        from_mp(emb_z, z_s, z_r, k).wait_recv()
-        block_sum = block_sum + emb_z[lax.rem(m + k, mp)].astype(F32)
-    for j in range(mp):
-        embedded[j] = block_sum[j * rows : (j + 1) * rows]
 
     gain = ln_gain[...].reshape(1, cols)
     normed = (gain * (block_sum - first_mean) * first_scale).astype(BF16)
@@ -322,7 +359,23 @@
         row_var = to_column(stats[1:2], rows) - row_mean * row_mean
         pieces.append(gain * (hid[j] - row_mean) * lax.rsqrt(row_var + EPS))
     fin[d] = jnp.concatenate(pieces, axis=0).astype(BF16)
-    fin_sends = [over_dp(lambda j: fin.at[d], fin, fin_s, fin_r, k) for k in range(1, dp)]
+    core = lax.rem(d, 2)
+    chip = d // 2
+    partner = d + 1 - 2 * core
+    swap = 1 - 2 * core
+
+    def fin_copy(slot, target, index):
+        return pltpu.make_async_remote_copy(
+            src_ref=fin.at[slot],
+            dst_ref=fin.at[slot],
+            send_sem=fin_s.at[index],
+            recv_sem=fin_r.at[slot],
+            device_id=(target, m),
+            device_id_type=MESH,
+        )
+
+    others = [2 * lax.rem(chip + k, dp // 2) + core for k in range(1, dp // 2)]
+    fin_sends = [fin_copy(d, other, other) for other in others] + [fin_copy(d, partner, partner)]
     for copy in fin_sends:
         copy.start()
 
@@ -333,9 +386,17 @@
         )
 
     logits = block_logits(d)
-    for k in range(1, dp):
-        from_dp(fin, fin_s, fin_r, k).wait_recv()
-        logits = logits + block_logits(lax.rem(d + k, dp))
+    fin_copy(partner, partner, partner).wait_recv()
+    logits = logits + block_logits(partner)
+    for other in others:
+        fin_copy(other, other, other).wait_recv()
+        passed = fin_copy(other, partner, other + swap)
+        passed.start()
+        fin_sends.append(passed)
+        logits = logits + block_logits(other)
+    for other in others:
+        fin_copy(other + swap, partner, partner).wait_recv()
+        logits = logits + block_logits(other + swap)
     local_top = jnp.max(logits, axis=-1, keepdims=True)
     local_sum = jnp.sum(jnp.exp(logits - local_top), axis=-1, keepdims=True)
     top[me] = jnp.concatenate([to_lanes(local_top), to_lanes(local_sum)], axis=0)
@@ -374,10 +435,12 @@
     cols = out_weight.shape[1]
     head_cols = query_weight.shape[1]
     rows = seqs // mp
+    chunks = next(k for k in (CHUNKS, 2, 1) if cols % (k * LANES) == 0)
+    wide = cols // chunks
     any_space = pl.BlockSpec(memory_space=pl.ANY)
     smem = pl.BlockSpec(memory_space=pltpu.SMEM)
     dma = pltpu.SemaphoreType.DMA
-    pairs = [dp, mp, n, dp, dp, mp, mp, n, dp, n]
+    pairs = [(chunks, dp), (chunks, mp)] + [(k,) for k in (n, dp, dp, mp, mp, n, dp, n)]
     return pl.pallas_call(
         functools.partial(kernel, dp, mp),
         out_shape=jax.ShapeDtypeStruct((seqs, embedding.shape[0]), F32),
@@ -391,9 +454,9 @@
             pltpu.VMEM(value_cache.shape, BF16),
             pltpu.VMEM(out_weight.shape, BF16),
             pltpu.VMEM((cols,), F32),
-            pltpu.VMEM((dp, seqs, cols), BF16),
-            pltpu.VMEM((dp, seqs, cols), BF16),
-            pltpu.VMEM((mp, seqs, cols), BF16),
+            pltpu.VMEM((chunks, dp, seqs, wide), BF16),
+            pltpu.VMEM((chunks, dp, seqs, wide), BF16),
+            pltpu.VMEM((chunks, mp, seqs, wide), BF16),
             pltpu.VMEM((n, 2, LANES), F32),
             pltpu.VMEM((mp, rows, cols), F32),
             pltpu.VMEM((dp, seq_here, head_cols), F32),
@@ -405,9 +468,11 @@
             pltpu.VMEM((n, 2, LANES), F32),
             pltpu.VMEM((dp, seqs, cols), BF16),
             pltpu.VMEM((n, 2, LANES), F32),
+            pltpu.SemaphoreType.REGULAR((max(mp - 2, 1),)),
+            pltpu.SemaphoreType.REGULAR,
             dma((7,)),
         ]
-        + [dma((size,)) for size in pairs for _ in range(2)],
+        + [dma(size) for size in pairs for _ in range(2)],
         compiler_params=pltpu.CompilerParams(
             collective_id=0, has_side_effects=True, vmem_limit_bytes=60 * 1024 * 1024
         ),

time: 57.3 us -> 53.1 us (0.927)
  Pallas kernels: 55.8 us -> 51.6 us
    pallas_call x1, Pallas kernels: 55.8 us -> 51.6 us  [per_device(): pl.pallas_call(functools.partial(kernel, dp, mp), out_shape=jax.ShapeDtyp...]
where the time goes in v2:
time: 53.1 us; the launch traced here: 52.9 us
  Pallas kernels  51.6 us (97%)
  local copies, waits for them, and re-layouts  1.3 us (2%)
    pallas_call x1, Pallas kernels, per_device(): pl.pallas_call(functools.partial(kernel, dp, mp), out_shape=jax.ShapeDtyp...  51.6 us
    unnamed x1, local copies, waits for them, and re-layouts  1.3 us

profile of v2, /device:TPU:0, one launch (start us, length us, event | category | flops | bytes accessed | tf_op | source)
XLA Modules:
  0.0 52.9 jit_solution(10901039514725238316)
XLA Ops:
  0.0 51.6 %shard_map.91 = f32[16,96]{1,0:T(8,128)} custom-call(s32[16]{0:T(128)} %tokens.1, s32[2]{0:T(128)} %lengths.1, bf16[96,12288]{1,0:T(8,128)(2,1)} %emb_hbm.1, f32[12288]{0:T(1024)} %ln_hbm.1, bf16[1536,1536]{1,0:T(8,128)(2,1)} %wq_hbm.1, bf16[2,512,1536]{2,1,0:T(8,128)(2,1)} %key_hbm.1, bf16[2,512,1536]{2,1,0:T(8,128)(2,1)} %val_hbm.1, ...), custom_call_target="tpu_custom_call" | custom-call | tf_op jit(solution)/shard_map/pallas_call | solution.py:444
  51.6 1.3 %copy.11 = f32[16,96]{1,0:T(8,128)} copy(f32[16,96]{1,0:T(8,128)} %shard_map.91) | data formatting | bytes 12288

commit v3 on v2

--- a/solution.py
+++ b/solution.py
@@ -133,8 +133,30 @@
         signal(barrier, lax.rem(d + k, dp), m)
     signal_line(barrier)
 
+    core = lax.rem(d, 2)
+    chip = d // 2
+    chips = dp // 2
+    partner = d + 1 - 2 * core
+    swap = 1 - 2 * core
+    corner = chips - 1 - chip
+    own = lax.rem(chip - corner + chips, chips)
+    chip_order = [lax.rem(corner + t + jnp.where(own <= t, 1, 0), chips) for t in range(chips - 1)]
+    others = [2 * c + core for c in chip_order]
+    far_dp = [j for other in others for j in (other, other + swap)] + [partner]
+    near_dp = far_dp[::-1]
+    upper = 2 * m >= mp
+    far_mp = [
+        jnp.where(
+            upper,
+            t + jnp.where(m <= t, 1, 0),
+            mp - 1 - t - jnp.where(mp - 1 - m <= t, 1, 0),
+        )
+        for t in range(mp - 1)
+    ]
+    near_mp = far_mp[::-1]
+
     def over_dp(src, dst, send, recv, k):
-        other = lax.rem(d + k, dp)
+        other = far_dp[k - 1]
         return pltpu.make_async_remote_copy(
             src_ref=src(other),
             dst_ref=dst.at[d],
@@ -145,7 +167,7 @@
         )
 
     def from_dp(dst, send, recv, k):
-        other = lax.rem(d + k, dp)
+        other = near_dp[k - 1]
         return pltpu.make_async_remote_copy(
             src_ref=dst.at[other],
             dst_ref=dst.at[other],
@@ -156,7 +178,7 @@
         )
 
     def over_mp(src, dst, send, recv, k):
-        other = lax.rem(m + k, mp)
+        other = far_mp[k - 1]
         return pltpu.make_async_remote_copy(
             src_ref=src(other),
             dst_ref=dst.at[m],
@@ -167,7 +189,7 @@
         )
 
     def from_mp(dst, send, recv, k):
-        other = lax.rem(m + k, mp)
+        other = near_mp[k - 1]
         return pltpu.make_async_remote_copy(
             src_ref=dst.at[other],
             dst_ref=dst.at[other],
@@ -257,7 +279,7 @@
         part_sum = emb_send[i, d].astype(F32)
         for k in range(1, dp):
             from_dp(emb_recv.at[i], emb_s.at[i], emb_r.at[i], k).wait_recv()
-            part_sum = part_sum + emb_recv[i, lax.rem(d + k, dp)].astype(F32)
+            part_sum = part_sum + emb_recv[i, near_dp[k - 1]].astype(F32)
         emb_z[i, m] = part_sum.astype(BF16)
         block_sums.append(part_sum)
         for k in range(1, mp):
@@ -272,7 +294,7 @@
     for i in range(chunks):
         for k in range(1, mp):
             from_mp(emb_z.at[i], z_s.at[i], z_r.at[i], k).wait_recv()
-            block_sums[i] = block_sums[i] + emb_z[i, lax.rem(m + k, mp)].astype(F32)
+            block_sums[i] = block_sums[i] + emb_z[i, near_mp[k - 1]].astype(F32)
     block_sum = jnp.concatenate(block_sums, axis=1)
     for j in range(mp):
         embedded[j] = block_sum[j * rows : (j + 1) * rows]
@@ -292,7 +314,7 @@
     query_sum = q_part[d]
     for k in range(1, dp):
         from_dp(q_recv, q_s, q_r, k).wait_recv()
-        query_sum = query_sum + q_recv[lax.rem(d + k, dp)]
+        query_sum = query_sum + q_recv[near_dp[k - 1]]
     queries = (query_sum * HD ** (-0.5)).astype(BF16).astype(F32)
 
     heads = heads_cols // HD
@@ -331,12 +353,9 @@
     mixed = o_part[m]
     for k in range(1, mp):
         from_mp(o_recv, o_s, o_r, k).wait_recv()
-        mixed = mixed + o_recv[lax.rem(m + k, mp)]
+        mixed = mixed + o_recv[near_mp[k - 1]]
     hidden = embedded[m] + mixed
     hid[m] = hidden
-    hid_sends = [over_mp(lambda j: hid.at[m], hid, hid_s, hid_r, k) for k in range(1, mp)]
-    for copy in hid_sends:
-        copy.start()
     stat2[me] = jnp.concatenate(
         [
             to_lanes(jnp.sum(hidden, axis=1, keepdims=True)),
@@ -345,6 +364,9 @@
         axis=0,
     )
     send_small(stat2, st2_s, st2_r)
+    hid_sends = [over_mp(lambda j: hid.at[m], hid, hid_s, hid_r, k) for k in range(1, mp)]
+    for copy in hid_sends:
+        copy.start()
     for k in range(1, mp):
         from_mp(hid, hid_s, hid_r, k).wait_recv()
     wait_small(stat2, st2_s, st2_r)
@@ -359,11 +381,6 @@
         row_var = to_column(stats[1:2], rows) - row_mean * row_mean
         pieces.append(gain * (hid[j] - row_mean) * lax.rsqrt(row_var + EPS))
     fin[d] = jnp.concatenate(pieces, axis=0).astype(BF16)
-    core = lax.rem(d, 2)
-    chip = d // 2
-    partner = d + 1 - 2 * core
-    swap = 1 - 2 * core
-
     def fin_copy(slot, target, index):
         return pltpu.make_async_remote_copy(
             src_ref=fin.at[slot],
@@ -374,7 +391,6 @@
             device_id_type=MESH,
         )
 
-    others = [2 * lax.rem(chip + k, dp // 2) + core for k in range(1, dp // 2)]
     fin_sends = [fin_copy(d, other, other) for other in others] + [fin_copy(d, partner, partner)]
     for copy in fin_sends:
         copy.start()
@@ -388,13 +404,13 @@
     logits = block_logits(d)
     fin_copy(partner, partner, partner).wait_recv()
     logits = logits + block_logits(partner)
-    for other in others:
+    for other in others[::-1]:
         fin_copy(other, other, other).wait_recv()
         passed = fin_copy(other, partner, other + swap)
         passed.start()
         fin_sends.append(passed)
         logits = logits + block_logits(other)
-    for other in others:
+    for other in others[::-1]:
         fin_copy(other + swap, partner, partner).wait_recv()
         logits = logits + block_logits(other + swap)
     local_top = jnp.max(logits, axis=-1, keepdims=True)

time: 53.1 us -> 52.1 us (0.981)
  Pallas kernels: 51.6 us -> 50.5 us
    pallas_call x1, Pallas kernels: 51.6 us -> 50.5 us  [per_device(): pl.pallas_call(functools.partial(kernel, dp, mp), out_shape=jax.ShapeDtyp...]
where the time goes in v3:
time: 52.1 us; the launch traced here: 51.9 us
  Pallas kernels  50.5 us (97%)
  local copies, waits for them, and re-layouts  1.3 us (2%)
    pallas_call x1, Pallas kernels, per_device(): pl.pallas_call(functools.partial(kernel, dp, mp), out_shape=jax.ShapeDtyp...  50.5 us
    unnamed x1, local copies, waits for them, and re-layouts  1.3 us

profile of v3, /device:TPU:0, one launch (start us, length us, event | category | flops | bytes accessed | tf_op | source)
XLA Modules:
  0.0 51.9 jit_solution(11261805046745482002)
XLA Ops:
  0.0 50.5 %shard_map.91 = f32[16,96]{1,0:T(8,128)} custom-call(s32[16]{0:T(128)} %tokens.1, s32[2]{0:T(128)} %lengths.1, bf16[96,12288]{1,0:T(8,128)(2,1)} %emb_hbm.1, f32[12288]{0:T(1024)} %ln_hbm.1, bf16[1536,1536]{1,0:T(8,128)(2,1)} %wq_hbm.1, bf16[2,512,1536]{2,1,0:T(8,128)(2,1)} %key_hbm.1, bf16[2,512,1536]{2,1,0:T(8,128)(2,1)} %val_hbm.1, ...), custom_call_target="tpu_custom_call" | custom-call | tf_op jit(solution)/shard_map/pallas_call | solution.py:460
  50.6 1.3 %copy.11 = f32[16,96]{1,0:T(8,128)} copy(f32[16,96]{1,0:T(8,128)} %shard_map.91) | data formatting | bytes 12288
